TPU v7x, 32 devices: a whole 2x2x4 slice. The times are simulated.
32 devices in a mesh: dp: 8 (over y, x, core), tensor: 4 (over z).
Axes of the slice: x: 2, y: 2, z: 4, core: 2. Of those that a mesh axis runs over, the one named last changes fastest.
Arguments:
- hidden_in: bfloat16 [4096, 2048], P('dp', 'tensor'), may hold values from -6 to 6
- cotangent: bfloat16 [4096, 2048], P('dp', 'tensor'), may hold values from -6 to 6
- segment_ids: int32 [4096], P('dp'), may hold values from -1 to 4095, as said below
- positions: int32 [4096], P('dp'), may hold values from 0 to 1023, as said below
- norm_gain: float32 [2048], replicated, may hold values from 0.25 to 1.75
- norm_shift: float32 [2048], replicated, may hold values from -1.5 to 1.5
- qkv_weight: bfloat16 [2048, 3, 2048], P(None, None, 'tensor'), may hold values from -0.53033009 to 0.53033009
- qv_bias: float32 [2, 2048], P(None, 'tensor'), may hold values from -3 to 3
- key_bias: float32 [32, 32], P('tensor'), may hold values from -3 to 3
- dense_weight: bfloat16 [2048, 2048], P('tensor'), may hold values from -1.5 to 1.5
- fc1_weight: bfloat16 [2048, 8192], P(None, 'tensor'), may hold values from -0.125 to 0.125
- fc1_bias: float32 [8192], P('tensor'), may hold values from -3 to 3
- fc2_weight: bfloat16 [8192, 2048], P('tensor'), may hold values from -0.0625 to 0.0625
- out_bias: float32 [2, 2048], replicated, may hold values from -1.5 to 1.5
Outputs:
- block_out: bfloat16 [4096, 2048], P('dp', 'tensor')
- input_grad: float32 [4096, 2048], P('dp', 'tensor')
- norm_grad: float32 [2, 2048], P(None, ('tensor', 'dp'))
- qkv_grad: float32 [2048, 3, 2048], P('dp', None, 'tensor')
- qvbias_grad: float32 [2, 2048], P(None, ('tensor', 'dp'))
- keybias_grad: float32 [32, 32], P('tensor', 'dp')
- dense_grad: float32 [2048, 2048], P(('tensor', 'dp'))
- fc1_grad: float32 [2048, 8192], P('dp', 'tensor')
- fc1bias_grad: float32 [8192], P(('tensor', 'dp'))
- fc2_grad: float32 [8192, 2048], P(('tensor', 'dp'))
- outbias_grad: float32 [2, 2048], P(None, ('tensor', 'dp'))
Inputs may be any that keep to these rules, and one draw needn't show every extreme that they name: `segment_ids`: the tokens of one segment id stand in a row inside one block of 512 slots, and different segments have different ids; -1 marks unused slots, which end a block; every block has 256 or more used slots, and some block is a single segment of 512 tokens. Within a segment the positions rise by one from token to token; unused slots have position 0.
All inputs are finite; a program needn't handle non-finite values.
Results may differ from a plain program's by a relative error of at most 0.028.
The roundings to bfloat16 on the way count: a program that leaves them out, or rounds other values in their place, can miss the bound.
Values may be sent and summed in bfloat16 or wider, within the bound.
A program may use at most 256 MiB of HBM per device.

v0:
```python
import jax
import jax.numpy as jnp
from jax import lax
from jax.sharding import PartitionSpec as P

HD = 64
ROT = 32


norm_epsilon = 1e-05
gelu_scale = 0.7978845608028654
gelu_cubic = 0.044715
masked_score = -1e30


def cut_along(shard, dim, devices):
    shape = shard.shape
    tiles = shard.reshape(*shape[:dim], devices, shape[dim] // devices, *shape[dim + 1 :])
    return jnp.moveaxis(tiles, dim, 0)


def summed_on_arrival(shard, axis, dim):
    devices = lax.axis_size(axis)
    tiles = lax.all_to_all(cut_along(shard, dim, devices), axis, 0, 0, tiled=True)
    return jnp.sum(tiles.astype(jnp.float32), axis=0)


def gelu_pair(pre_act):
    tanh_val = jnp.tanh(gelu_scale * (pre_act + gelu_cubic * pre_act * pre_act * pre_act))
    gelu_val = 0.5 * pre_act * (1.0 + tanh_val)
    gelu_slope = 0.5 * (1.0 + tanh_val) + 0.5 * pre_act * (
        1.0 - tanh_val * tanh_val
    ) * gelu_scale * (1.0 + 3.0 * gelu_cubic * pre_act * pre_act)
    return (gelu_val, gelu_slope)


def rotary_tables(positions, rot_dims):
    half_rot = rot_dims // 2
    exponent = jnp.arange(half_rot, dtype=jnp.float32) * (2.0 / rot_dims)
    inverse = jnp.power(jnp.float32(10000.0), -exponent)
    angles = positions.astype(jnp.float32)[:, None] * inverse[None, :]
    return (jnp.cos(angles)[:, None, :], jnp.sin(angles)[:, None, :])


def rotate_fwd(operand, cosine, sine, rot_dims):
    half_rot = rot_dims // 2
    lower = operand[..., :half_rot]
    upper = operand[..., half_rot:rot_dims]
    return jnp.concatenate(
        [lower * cosine - upper * sine, upper * cosine + lower * sine, operand[..., rot_dims:]],
        axis=-1,
    )


def rotate_back(operand, cosine, sine, rot_dims):
    half_rot = rot_dims // 2
    lower = operand[..., :half_rot]
    upper = operand[..., half_rot:rot_dims]
    return jnp.concatenate(
        [lower * cosine + upper * sine, upper * cosine - lower * sine, operand[..., rot_dims:]],
        axis=-1,
    )


def per_device(
    hidden_in,
    cotangent,
    segment_ids,
    positions,
    norm_gain,
    norm_shift,
    qkv_weight,
    qv_bias,
    key_bias,
    dense_weight,
    fc1_weight,
    fc1_bias,
    fc2_weight,
    out_bias,
):
    tok_rows = hidden_in.shape[0]
    width_loc = hidden_in.shape[1]
    heads_loc = key_bias.shape[0]
    score_scale = HD ** (-0.5)
    col_start = lax.axis_index("tensor") * width_loc
    full_in, full_cot = (
        lax.all_gather(hidden_in, "tensor", axis=1, tiled=True),
        lax.all_gather(cotangent, "tensor", axis=1, tiled=True),
    )
    in_f = full_in.astype(jnp.float32)
    row_mean = jnp.mean(in_f, axis=1, keepdims=True)
    centred = in_f - row_mean
    inv_std = lax.rsqrt(jnp.mean(centred * centred, axis=1, keepdims=True) + norm_epsilon)
    normed = centred * inv_std
    hidden = (normed * norm_gain + norm_shift).astype(jnp.bfloat16)
    projected = jnp.einsum("td,dcn->tcn", hidden, qkv_weight, preferred_element_type=jnp.float32)
    cosine, sine = rotary_tables(positions, ROT)
    key_pad = jnp.concatenate([key_bias, jnp.zeros((heads_loc, HD - ROT), jnp.float32)], axis=1)
    queries = rotate_fwd(
        (projected[:, 0] + qv_bias[0]).reshape(tok_rows, heads_loc, HD), cosine, sine, ROT
    ).astype(jnp.bfloat16)
    keys_rot = rotate_fwd(
        projected[:, 1].reshape(tok_rows, heads_loc, HD) + key_pad[None], cosine, sine, ROT
    ).astype(jnp.bfloat16)
    values_b = (projected[:, 2] + qv_bias[1]).reshape(tok_rows, heads_loc, HD).astype(jnp.bfloat16)
    blk_rows = min(512, tok_rows)
    blk_starts = jnp.arange(tok_rows // blk_rows, dtype=jnp.int32) * blk_rows
    slot_ids = jnp.arange(tok_rows, dtype=jnp.int32)

    def block_scores(row_start):
        own_slots = row_start + jnp.arange(blk_rows, dtype=jnp.int32)
        allowed = (segment_ids[:, None] == segment_ids[None, :]) & (
            slot_ids[None, :] <= own_slots[:, None]
        )
        raw_scores = (
            jnp.einsum("qhd,khd->hqk", queries, keys_rot, preferred_element_type=jnp.float32)
            * score_scale
        )
        return (jnp.where(allowed[None], raw_scores, masked_score), queries)

    def forward_block(row_start):
        scores, q_block = block_scores(row_start)
        row_top = jnp.max(scores, axis=2, keepdims=True)
        log_total = row_top + jnp.log(jnp.sum(jnp.exp(scores - row_top), axis=2, keepdims=True))
        prob_b = jnp.exp(scores - log_total).astype(jnp.bfloat16)
        mixed_block = jnp.einsum(
            "hqk,khd->qhd", prob_b, values_b, preferred_element_type=jnp.float32
        ).astype(jnp.bfloat16)
        return (mixed_block, log_total[:, :, 0])

    mixed_all, log_totals = lax.map(forward_block, blk_starts)
    attn_mix = mixed_all.reshape(tok_rows, heads_loc, HD)
    attn_flat = attn_mix.reshape(tok_rows, heads_loc * HD)
    pre_act = jnp.dot(hidden, fc1_weight, preferred_element_type=jnp.float32) + fc1_bias
    gelu_val, gelu_slope = gelu_pair(pre_act)
    act_b = gelu_val.astype(jnp.bfloat16)
    partial_out = jnp.dot(attn_flat, dense_weight, preferred_element_type=jnp.float32) + jnp.dot(
        act_b, fc2_weight, preferred_element_type=jnp.float32
    )
    summed_out = summed_on_arrival(partial_out.astype(jnp.bfloat16), "tensor", 1)
    bias_loc = lax.dynamic_slice_in_dim(out_bias[0] + out_bias[1], col_start, width_loc, 0)
    block_out = (hidden_in.astype(jnp.float32) + summed_out + bias_loc).astype(jnp.bfloat16)
    live_rows = segment_ids >= 0
    grad_b = jnp.where(live_rows[:, None], full_cot, jnp.zeros_like(full_cot))
    fc2_g = jnp.einsum("tf,td->fd", act_b, grad_b, preferred_element_type=jnp.float32)
    dense_g = jnp.einsum("tn,td->nd", attn_flat, grad_b, preferred_element_type=jnp.float32)
    col_sums = lax.dynamic_slice_in_dim(
        jnp.sum(grad_b.astype(jnp.float32), axis=0), col_start, width_loc, 0
    )
    outb_g = jnp.stack([col_sums, col_sums])
    d_pre = (
        jnp.einsum("td,fd->tf", grad_b, fc2_weight, preferred_element_type=jnp.float32) * gelu_slope
    )
    d_pre_b = d_pre.astype(jnp.bfloat16)
    fc1_g = jnp.einsum("td,tf->df", hidden, d_pre_b, preferred_element_type=jnp.float32)
    fc1b_g = jnp.sum(d_pre, axis=0)
    d_attn = (
        jnp.einsum("td,nd->tn", grad_b, dense_weight, preferred_element_type=jnp.float32)
        .astype(jnp.bfloat16)
        .reshape(tok_rows, heads_loc, HD)
    )
    delta_all = jnp.sum(d_attn.astype(jnp.float32) * attn_mix.astype(jnp.float32), axis=2)

    def backward_block(accums, inputs):
        row_start, log_block = inputs
        dk_acc, dv_acc = accums
        scores, q_block = block_scores(row_start)
        prob_f = jnp.exp(scores - log_block[:, :, None])
        prob_b = prob_f.astype(jnp.bfloat16)
        d_prob = jnp.einsum("qhd,khd->hqk", d_attn, values_b, preferred_element_type=jnp.float32)
        d_score = (prob_f * (d_prob - delta_all.T[:, :, None]) * score_scale).astype(jnp.bfloat16)
        dq_block = jnp.einsum("hqk,khd->qhd", d_score, keys_rot, preferred_element_type=jnp.float32)
        dk_acc = dk_acc + jnp.einsum(
            "hqk,qhd->khd", d_score, q_block, preferred_element_type=jnp.float32
        )
        dv_acc = dv_acc + jnp.einsum(
            "hqk,qhd->khd", prob_b, d_attn, preferred_element_type=jnp.float32
        )
        return ((dk_acc, dv_acc), dq_block)

    zero_acc = jnp.zeros((tok_rows, heads_loc, HD), jnp.float32)
    (d_key, d_value), dq_all = lax.scan(
        backward_block, (zero_acc, zero_acc), (blk_starts, log_totals)
    )
    d_query = rotate_back(dq_all.reshape(tok_rows, heads_loc, HD), cosine, sine, ROT).reshape(
        tok_rows, width_loc
    )
    d_key = rotate_back(d_key, cosine, sine, ROT)
    keyb_g = jnp.sum(d_key[:, :, :ROT], axis=0)
    d_key = d_key.reshape(tok_rows, width_loc)
    d_value = d_value.reshape(tok_rows, width_loc)
    qvb_g = jnp.stack([jnp.sum(d_query, axis=0), jnp.sum(d_value, axis=0)])
    d_proj = jnp.stack([d_query, d_key, d_value], axis=1).astype(jnp.bfloat16)
    qkv_g = jnp.einsum("td,tcn->dcn", hidden, d_proj, preferred_element_type=jnp.float32)
    dh_part = jnp.einsum(
        "tcn,dcn->td", d_proj, qkv_weight, preferred_element_type=jnp.float32
    ) + jnp.einsum("tf,df->td", d_pre_b, fc1_weight, preferred_element_type=jnp.float32)
    normed_loc = lax.dynamic_slice_in_dim(normed, col_start, width_loc, 1)
    dh_full = lax.psum(dh_part.astype(jnp.bfloat16), "tensor").astype(jnp.float32)
    scaled = dh_full * norm_gain
    dx_full = inv_std * (
        scaled
        - jnp.mean(scaled, axis=1, keepdims=True)
        - normed * jnp.mean(scaled * normed, axis=1, keepdims=True)
    )
    dx_loc = lax.dynamic_slice_in_dim(dx_full, col_start, width_loc, 1)
    dh_loc = lax.dynamic_slice_in_dim(dh_full, col_start, width_loc, 1)
    own_grad = jnp.where(live_rows[:, None], cotangent, jnp.zeros_like(cotangent)).astype(
        jnp.float32
    )
    input_grad = dx_loc + own_grad
    norm_g = jnp.stack([jnp.sum(dh_loc * normed_loc, axis=0), jnp.sum(dh_loc, axis=0)])
    qkv_sh, qvb_sh, keyb_sh, norm_sh, fc2_sh, dense_sh, fc1_sh, fc1b_sh, outb_sh = (
        lax.psum_scatter(qkv_g.astype(jnp.bfloat16), "dp", scatter_dimension=0, tiled=True).astype(
            jnp.float32
        ),
        lax.psum_scatter(qvb_g.astype(jnp.bfloat16), "dp", scatter_dimension=1, tiled=True).astype(
            jnp.float32
        ),
        lax.psum_scatter(keyb_g.astype(jnp.bfloat16), "dp", scatter_dimension=1, tiled=True).astype(
            jnp.float32
        ),
        lax.psum_scatter(norm_g.astype(jnp.bfloat16), "dp", scatter_dimension=1, tiled=True).astype(
            jnp.float32
        ),
        lax.psum_scatter(fc2_g.astype(jnp.bfloat16), "dp", scatter_dimension=0, tiled=True).astype(
            jnp.float32
        ),
        lax.psum_scatter(
            dense_g.astype(jnp.bfloat16), "dp", scatter_dimension=0, tiled=True
        ).astype(jnp.float32),
        lax.psum_scatter(fc1_g.astype(jnp.bfloat16), "dp", scatter_dimension=0, tiled=True).astype(
            jnp.float32
        ),
        lax.psum_scatter(fc1b_g.astype(jnp.bfloat16), "dp", scatter_dimension=0, tiled=True).astype(
            jnp.float32
        ),
        lax.psum_scatter(outb_g.astype(jnp.bfloat16), "dp", scatter_dimension=1, tiled=True).astype(
            jnp.float32
        ),
    )
    return (
        block_out,
        input_grad,
        norm_sh,
        qkv_sh,
        qvb_sh,
        keyb_sh,
        dense_sh,
        fc1_sh,
        fc1b_sh,
        fc2_sh,
        outb_sh,
    )


def solution(mesh):
    placed = (
        P("dp", "tensor"),
        P("dp", "tensor"),
        P("dp"),
        P("dp"),
        P(),
        P(),
        P(None, None, "tensor"),
        P(None, "tensor"),
        P("tensor", None),
        P("tensor", None),
        P(None, "tensor"),
        P("tensor"),
        P("tensor", None),
        P(),
    )
    return jax.shard_map(
        per_device,
        mesh=mesh,
        in_specs=placed,
        out_specs=(
            P("dp", "tensor"),
            P("dp", "tensor"),
            P(None, ("tensor", "dp")),
            P("dp", None, "tensor"),
            P(None, ("tensor", "dp")),
            P("tensor", "dp"),
            P(("tensor", "dp"), None),
            P("dp", "tensor"),
            P(("tensor", "dp")),
            P(("tensor", "dp"), None),
            P(None, ("tensor", "dp")),
        ),
        check_vma=False,
    )
```

profile of v0, /device:TPU:0, one launch (start us, length us, event | category | flops | bytes accessed | tf_op | source)
XLA Modules:
  0.0 639.7 jit_solution(14329960169093850460)
XLA Ops:
  12.9 45.1 %all-gather.3.cloned.1.call-done = bf16[512,2048]{1,0:T(8,128)(2,1)} async-done(((bf16[512,512]{1,0:T(8,128)(2,1)}), bf16[512,2048]{1,0:T(8,128)(2,1)}) %all-gather.3.cloned.1.call-update) | async-done | bytes 2097168 | tf_op jit(solution)/shard_map/all_gather | solution.py:87
  62.4 6.0 fusion.13
  74.9 29.1 %all-gather.5.cloned.1.call-done = bf16[512,2048]{1,0:T(8,128)(2,1)} async-done(((bf16[512,512]{1,0:T(8,128)(2,1)}), bf16[512,2048]{1,0:T(8,128)(2,1)}) %all-gather.5.cloned.1.call-update) | async-done | bytes 2097168 | tf_op jit(solution)/shard_map/all_gather | solution.py:88
  107.2 6.7 %multiply_reduce_fusion.2 = (f32[512,8]{0,1:T(8,128)S(1)}, bf16[8,64,512]{2,1,0:T(8,128)(2,1)}) fusion(bf16[512,512]{0,1:T(8,128)(2,1)S(1)} %convolution_convert_fusion.4, f32[8,512,512]{1,2,0:T(8,128)} %copy-done.2, f32[8,512]{1,0:T(8,128)S(1)} %log_add_fusion, pred[512,512]{0,1:T(8,128)(4,1)S(1)} %fusion.22, f32[512,8,64]{0,2,1:T(8,128)S(1)} %bitcast.70, ...), kind=kOutput, calls=%fused_computation.53 | convolution fusion | flops 278654976 | bytes 10782720 | tf_op jit(solution)/shard_map/while/body/eval_jaxpr/hqk,khd->qhd/dot_general | solution.py:126
  113.9 15.1 %multiply_convert_fusion = bf16[8,512,512]{1,2,0:T(8,128)(2,1)S(1)} fusion(f32[8,512,512]{1,2,0:T(8,128)S(1)} %bitcast.62, f32[8,512]{1,0:T(8,128)S(1)} %bitcast.84, f32[8,512]{1,0:T(8,128)S(1)} %log_add_fusion, pred[512,512]{0,1:T(8,128)(4,1)S(1)} %fusion.22, bf16[512,8,64]{0,2,1:T(8,128)(2,1)S(1)} %bitcast.82, f32[512,8,64]{0,2,1:T(8,128)S(1)} %bitcast.71, ...), kind=kOutput, calls=%fused_computation | convolution fusion | flops 283639808 | bytes 14452736 | tf_op jit(solution)/shard_map/while/body/eval_jaxpr/qhd,khd->hqk/dot_general | solution.py:170
  131.2 3.1 fusion.38
  142.6 7.8 %fusion.34 = f32[512,2048]{1,0:T(8,128)S(1)} fusion(bf16[2048,2048]{1,0:T(8,128)(2,1)} %param.24, f32[2048]{0:T(1024)S(1)} %copy-done.16, f32[2048]{0:T(1024)S(1)} %copy-done.15, f32[512]{0:T(512)S(1)} %add_rsqrt_fusion, f32[512]{0:T(512)S(1)} %broadcast_multiply_fusion.3, bf16[512,2048]{1,0:T(8,128)(2,1)} %all-gather.3.cloned.1.call-done), kind=kOutput, calls=%fused_computation.103 | convolution fusion | flops 4301258752 | bytes 14700544 | tf_op jit(solution)/shard_map/dot_general | solution.py:134
  150.4 13.0 %fusion.40 = (bf16[2048]{0:T(1024)(128)(2,1)S(1)}, bf16[512,2048]{1,0:T(8,128)(2,1)}) fusion(f32[512,2048]{1,0:T(8,128)S(1)} %fusion.34, f32[2048]{0:T(1024)S(1)} %copy-done.17, bf16[2048,2048]{1,0:T(8,128)(2,1)} %param.26, bf16[512,2048]{1,0:T(8,128)(2,1)S(1)} %copy-done.5, pred[512]{0:T(512)(128)(4,1)S(1)} %broadcast_compare_fusion), kind=kOutput, calls=%fused_computation.109 | convolution fusion | flops 4318033920 | bytes 16790016 | tf_op jit(solution)/shard_map/td,fd->tf/dot_general | solution.py:152
  163.5 7.7 %fusion.20 = f32[512,2048]{1,0:T(8,128)S(1)} fusion(bf16[2048,2048]{1,0:T(8,128)(2,1)} %param.24, bf16[512,2048]{1,0:T(8,128)(2,1)} %get-tuple-element.115), kind=kOutput, calls=%fused_computation.51 | convolution fusion | flops 4294967296 | bytes 14680064 | tf_op jit(solution)/shard_map/tf,df->td/dot_general | solution.py:197
  171.3 4.7 fusion.11
  180.8 80.3 %all-reduce.6.cloned.1.call-done = bf16[512,2048]{1,0:T(8,128)(2,1)} async-done(((bf16[512,2048]{1,0:T(8,128)(2,1)}), bf16[512,2048]{1,0:T(8,128)(2,1)}) %all-reduce.6.cloned.1.call-update) | async-done | bytes 2097168 | tf_op jit(solution)/shard_map/psum | solution.py:199
  261.1 3.7 fusion.18
  268.2 4.3 convolution_convert_fusion.3
  272.6 8.2 %convolution_convert_fusion.2 = bf16[2048,3,512]{2,0,1:T(8,128)(2,1)} fusion(bf16[512,1,512]{2,0,1:T(8,128)(2,1)} %copy.44, bf16[512,1,512]{2,0,1:T(8,128)(2,1)} %copy.43, bf16[512,1,512]{2,0,1:T(8,128)(2,1)S(1)} %copy-done.11, f32[2048]{0:T(1024)S(1)} %copy-done.16, f32[2048]{0:T(1024)S(1)} %copy-done.15, f32[512]{0:T(512)S(1)} %add_rsqrt_fusion, ...), kind=kOutput, calls=%fused_computation.14 | convolution fusion | flops 3235381248 | bytes 9981952 | tf_op jit(solution)/shard_map/td,tcn->dcn/dot_general | solution.py:194
  280.8 10.2 %convolution_convert_fusion.1 = bf16[2048,2048]{1,0:T(8,128)(2,1)} fusion(bf16[512,2048]{1,0:T(8,128)(2,1)} %get-tuple-element.115, f32[2048]{0:T(1024)S(1)} %copy-done.16, f32[2048]{0:T(1024)S(1)} %copy-done.15, f32[512]{0:T(512)S(1)} %add_rsqrt_fusion, f32[512]{0:T(512)S(1)} %broadcast_multiply_fusion.3, bf16[512,2048]{1,0:T(8,128)(2,1)} %all-gather.3.cloned.1.call-done), kind=kOutput, calls=%fused_computation.5 | convolution fusion | flops 4305453056 | bytes 12603392 | tf_op jit(solution)/shard_map/td,tf->df/dot_general | solution.py:155
  291.3 11.7 %convolution_convert_fusion = bf16[2048,2048]{1,0:T(8,128)(2,1)} fusion(f32[512,2048]{1,0:T(8,128)} %copy-done.19, f32[2048]{0:T(1024)S(1)} %copy-done.17, bf16[512,2048]{1,0:T(8,128)(2,1)} %all-gather.5.cloned.1.call-done, pred[512]{0:T(512)(128)(4,1)S(1)} %broadcast_compare_fusion), kind=kOutput, calls=%fused_computation.4 | convolution fusion | flops 4310695936 | bytes 14688768 | tf_op jit(solution)/shard_map/tf,td->fd/dot_general | solution.py:145
  303.0 9.1 %fusion.33 = f32[512,2048]{1,0:T(8,128)S(1)} fusion(bf16[2048,2048]{1,0:T(8,128)(2,1)} %param.26, f32[512,2048]{1,0:T(8,128)} %copy-done.19, f32[2048]{0:T(1024)S(1)} %copy-done.17), kind=kOutput, calls=%fused_computation.102 | convolution fusion | flops 4305453056 | bytes 16785408 | tf_op jit(solution)/shard_map/dot_general | solution.py:137
  314.9 4.6 all-to-all-start
  321.7 24.4 %all-reduce.3 = (bf16[8,32]{0,1:T(8,128)(2,1)S(1)}, bf16[2048]{0:T(1024)(128)(2,1)S(1)}) all-reduce(bf16[8,32]{0,1:T(8,128)(2,1)S(1)} %copy.46, bf16[2048]{0:T(1024)(128)(2,1)S(1)} %get-tuple-element.114), channel_id=5, replica_groups=mesh['dp'=8,'tensor'=4] {'dp'}, use_global_device_ids=true, to_apply=%region_17.18.clone | all-reduce | flops 2304 | bytes 9216
  350.1 19.9 %reduce-scatter.22.cloned.1.call-done = bf16[64,2]{1,0:T(8,128)(2,1)} async-done(((bf16[512,2]{1,0:T(8,128)(2,1)}), bf16[64,2]{1,0:T(8,128)(2,1)}) %reduce-scatter.22.cloned.1.call-update) | async-done | bytes 272
  371.4 43.6 %reduce-scatter.16.cloned.1.call-done = bf16[64,2048]{1,0:T(8,128)(2,1)} async-done(((bf16[512,2048]{1,0:T(8,128)(2,1)}), bf16[64,2048]{1,0:T(8,128)(2,1)}) %reduce-scatter.16.cloned.1.call-update) | async-done | bytes 262160 | tf_op jit(solution)/shard_map/reduce_scatter | solution.py:229
  419.8 60.3 %reduce-scatter.14.cloned.1.call-done = bf16[256,3,512]{2,0,1:T(8,128)(2,1)} async-done(((bf16[2048,3,512]{2,0,1:T(8,128)(2,1)}), bf16[256,3,512]{2,0,1:T(8,128)(2,1)}) %reduce-scatter.14.cloned.1.call-update) | async-done | bytes 786448 | tf_op jit(solution)/shard_map/reduce_scatter | solution.py:214
  482.6 72.5 %reduce-scatter.18.cloned.1.call-done = bf16[256,2048]{1,0:T(8,128)(2,1)} async-done(((bf16[2048,2048]{1,0:T(8,128)(2,1)}), bf16[256,2048]{1,0:T(8,128)(2,1)}) %reduce-scatter.18.cloned.1.call-update) | async-done | bytes 1048592 | tf_op jit(solution)/shard_map/reduce_scatter | solution.py:232
  557.9 72.0 %reduce-scatter.20.cloned.1.call-done = bf16[256,2048]{1,0:T(8,128)(2,1)} async-done(((bf16[2048,2048]{1,0:T(8,128)(2,1)}), bf16[256,2048]{1,0:T(8,128)(2,1)}) %reduce-scatter.20.cloned.1.call-update) | async-done | bytes 1048592 | tf_op jit(solution)/shard_map/reduce_scatter | solution.py:226
  (144 shorter events, 60.4 us)
Async XLA Ops:
  7.2 96.9 %copy-start = (bf16[512,2048]{1,0:T(8,128)(2,1)S(1)}, bf16[512,2048]{1,0:T(8,128)(2,1)}, u32[]{:S(2)}) copy-start(bf16[512,2048]{1,0:T(8,128)(2,1)} %param.23) | copy-start | bytes 6291460
  7.2 55.2 %copy-start.15 = (f32[2048]{0:T(1024)S(1)}, f32[2048]{0:T(1024)}, u32[]{:S(2)}) copy-start(f32[2048]{0:T(1024)} %param.18) | copy-start | bytes 24580
  7.2 55.2 %copy-start.16 = (f32[2048]{0:T(1024)S(1)}, f32[2048]{0:T(1024)}, u32[]{:S(2)}) copy-start(f32[2048]{0:T(1024)} %param.19) | copy-start | bytes 24580
  7.2 50.8 %all-gather.3.cloned.1.call-start = ((), (), s32[]{:S(2)}) async-start(), calls=%async_computation.8 | async-start | bytes 2621440 | tf_op jit(solution)/shard_map/all_gather | solution.py:87
  7.9 96.1 %all-gather.5.cloned.1.call-start = ((), (), s32[]{:S(2)}) async-start(), calls=%async_computation.9 | async-start | bytes 2621440 | tf_op jit(solution)/shard_map/all_gather | solution.py:88
  8.7 252.4 %all-reduce.6.cloned.1.call-start = ((), (), s32[]{:S(2)}) async-start(), calls=%async_computation.10 | async-start | bytes 4194304 | tf_op jit(solution)/shard_map/psum | solution.py:199
  104.1 9.8 %slice-start = ((s8[8388608]{0:T(1024)(128)(4,1)}), s8[4194304]{0:T(1024)(128)(4,1)S(1)}, s32[]{:S(2)}) async-start(s8[8388608]{0:T(1024)(128)(4,1)} %bitcast.61), calls=%async_computation.18 | async-start | bytes 8388608
  142.6 7.8 %copy-start.5 = (bf16[512,2048]{1,0:T(8,128)(2,1)S(1)}, bf16[512,2048]{1,0:T(8,128)(2,1)}, u32[]{:S(2)}) copy-start(bf16[512,2048]{1,0:T(8,128)(2,1)} %all-gather.5.cloned.1.call-done) | copy-start | bytes 6291460
  142.6 7.8 %copy-start.17 = (f32[2048]{0:T(1024)S(1)}, f32[2048]{0:T(1024)}, u32[]{:S(2)}) copy-start(f32[2048]{0:T(1024)} %param.25) | copy-start | bytes 24580
  142.6 28.7 %slice-start.2 = ((s8[6291456]{0:T(1024)(128)(4,1)}), s8[4194304]{0:T(1024)(128)(4,1)S(1)}, s32[]{:S(2)}) async-start(s8[6291456]{0:T(1024)(128)(4,1)} %bitcast.80), calls=%async_computation.20 | async-start | bytes 8388608
  150.4 13.1 %copy-start.19 = (f32[512,2048]{1,0:T(8,128)}, f32[512,2048]{1,0:T(8,128)S(1)}, u32[]{:S(2)}) copy-start(f32[512,2048]{1,0:T(8,128)S(1)} %fusion.34) | copy-start | bytes 12582916
  150.4 20.8 %slice-start.3 = ((s8[6291456]{0:T(1024)(128)(4,1)}), s8[2097152]{0:T(1024)(128)(4,1)S(1)}, s32[]{:S(2)}) async-start(s8[6291456]{0:T(1024)(128)(4,1)} %bitcast.80), calls=%async_computation.21 | async-start | bytes 4194304
  163.5 7.8 %copy-start.13 = (bf16[512,1,512]{2,0,1:T(8,128)(2,1)S(1)}, bf16[512,1,512]{2,0,1:T(8,128)(2,1)}, u32[]{:S(2)}) copy-start(bf16[512,1,512]{2,0,1:T(8,128)(2,1)} %copy.44) | copy-start | bytes 1572868
  176.0 171.4 %reduce-scatter.24.cloned.1.call-start = ((), (), s32[]{:S(2)}) async-start(), calls=%async_computation.16 | async-start | bytes 147456
  179.4 169.3 %reduce-scatter.26.cloned.1.call-start = ((), (), s32[]{:S(2)}) async-start(), calls=%async_computation.17 | async-start | bytes 147456
  180.3 189.7 %reduce-scatter.22.cloned.1.call-start = ((), (), s32[]{:S(2)}) async-start(), calls=%async_computation.15 | async-start | bytes 147456
  268.1 146.9 %reduce-scatter.16.cloned.1.call-start = ((), (), s32[]{:S(2)}) async-start(), calls=%async_computation.12 | async-start | bytes 2359296 | tf_op jit(solution)/shard_map/reduce_scatter | solution.py:229
  272.5 207.6 %reduce-scatter.14.cloned.1.call-start = ((), (), s32[]{:S(2)}) async-start(), calls=%async_computation.11 | async-start | bytes 7077888 | tf_op jit(solution)/shard_map/reduce_scatter | solution.py:214
  280.8 274.3 %reduce-scatter.18.cloned.1.call-start = ((), (), s32[]{:S(2)}) async-start(), calls=%async_computation.13 | async-start | bytes 9437184 | tf_op jit(solution)/shard_map/reduce_scatter | solution.py:232
  291.1 338.9 %reduce-scatter.20.cloned.1.call-start = ((), (), s32[]{:S(2)}) async-start(), calls=%async_computation.14 | async-start | bytes 9437184 | tf_op jit(solution)/shard_map/reduce_scatter | solution.py:226
  313.4 8.0 %copy-start.14 = (f32[2,2048]{1,0:T(2,128)S(1)}, f32[2,2048]{1,0:T(2,128)}, u32[]{:S(2)}) copy-start(f32[2,2048]{1,0:T(2,128)} %param.27) | copy-start | bytes 49156
  313.4 8.1 %copy-start.8 = (f32[512,8,16]{0,2,1:T(8,128)S(1)}, f32[512,8,16]{0,2,1:T(8,128)}, u32[]{:S(2)}) copy-start(f32[512,8,16]{0,2,1:T(8,128)} %get-tuple-element.102) | copy-start | bytes 786436
  314.9 103.9 %copy-start.4 = (bf16[512,512]{1,0:T(8,128)(2,1)S(1)}, bf16[512,512]{1,0:T(8,128)(2,1)}, u32[]{:S(2)}) copy-start(bf16[512,512]{1,0:T(8,128)(2,1)} %param.14) | copy-start | bytes 1572868
  314.9 101.8 %all-to-all-start = ((bf16[4,512,512]{2,1,0:T(8,128)(2,1)}), bf16[4,512,512]{2,1,0:T(8,128)(2,1)}, u32[]{:S(2)}, u32[]{:S(2)}) async-start(bf16[4,512,512]{2,1,0:T(8,128)(2,1)} %bitcast.63), calls=%async_computation | async-start | bytes 4194304 | tf_op jit(solution)/shard_map/all_to_all | solution.py:24
  (11 other events, 51.6 us)
Sparse Core Ops, SparseCore 0:
  9.6 48.3 all-gather.2
  59.6 44.4 all-gather.4
  176.1 84.9 all-reduce.5
  264.0 32.5 reduce-scatter.23
  299.4 33.5 reduce-scatter.25
  336.4 33.5 reduce-scatter.21
  373.9 41.0 reduce-scatter.15
  418.4 61.6 reduce-scatter.13
  483.6 71.4 reduce-scatter.17
  558.4 71.4 reduce-scatter.19
where the time goes:
time: 644 us; the launch traced here: 640 us
  waiting for transfers between devices  424 us (66%)
  matrix products  116 us (18%)
  other arithmetic  34.8 us (5%)
  blocking collectives  24.4 us (4%)
  local copies, waits for them, and re-layouts  18.5 us (3%)
  between operations  16.2 us (3%)
    psum x1, waiting for transfers between devices, per_device(): lax.psum(dh_part.astype(jnp.bfloat16), 'tensor').astype(jnp.float32)  80.3 us
    reduce_scatter x1, waiting for transfers between devices, per_device(): lax.psum_scatter(fc1_g.astype(jnp.bfloat16), 'dp', scatter_dimension=0, t...  72.5 us
    reduce_scatter x1, waiting for transfers between devices, per_device(): lax.psum_scatter(fc2_g.astype(jnp.bfloat16), 'dp', scatter_dimension=0, t...  72 us
    reduce_scatter x1, waiting for transfers between devices, per_device(): lax.psum_scatter(qkv_g.astype(jnp.bfloat16), 'dp', scatter_dimension=0, t...  60.3 us
    all_gather x1, waiting for transfers between devices, per_device(): lax.all_gather(hidden_in, 'tensor', axis=1, tiled=True)  45.1 us
    reduce_scatter x1, waiting for transfers between devices, per_device(): lax.psum_scatter(dense_g.astype(jnp.bfloat16), 'dp', scatter_dimension=0,...  43.6 us
    all_gather x1, waiting for transfers between devices, per_device(): lax.all_gather(cotangent, 'tensor', axis=1, tiled=True)  29.1 us
    unnamed x1, blocking collectives  24.4 us
  transfers between devices with their start and end apart: 11, of which 8 were waited for; matrix products, arithmetic and copies ran while one was open for 14% of the time, Pallas kernels for 0%

commit v1 on v0

v1 whole, which is shorter than its diff:
```python
import functools

import jax
import jax.numpy as jnp
from jax import lax
from jax.experimental import pallas as pl
from jax.experimental.pallas import tpu as pltpu
from jax.sharding import PartitionSpec as P

HD = 64
ROT = 32
LANES = 128

norm_epsilon = 1e-05
gelu_scale = 0.7978845608028654
gelu_cubic = 0.044715
masked_score = -1e30

MESH = pl.DeviceIdType.MESH
F32 = jnp.float32
BF16 = jnp.bfloat16
VMEM_BYTES = 67043328


def gelu_pair(pre_act):
    tanh_val = jnp.tanh(gelu_scale * (pre_act + gelu_cubic * pre_act * pre_act * pre_act))
    gelu_val = 0.5 * pre_act * (1.0 + tanh_val)
    gelu_slope = 0.5 * (1.0 + tanh_val) + 0.5 * pre_act * (
        1.0 - tanh_val * tanh_val
    ) * gelu_scale * (1.0 + 3.0 * gelu_cubic * pre_act * pre_act)
    return (gelu_val, gelu_slope)


class Place:
    def __init__(self, nd, nt):
        self.nd, self.nt = nd, nt
        self.nch = nd // 2
        self.bits = self.nch.bit_length() - 1
        self.d = lax.axis_index("dp")
        self.t = lax.axis_index("tensor")
        self.c = lax.rem(self.d, 2)
        self.j = self.d // 2

    def pair(self):
        return (self.d + 1 - 2 * self.c, self.t)

    def chip_bit(self, b):
        return lax.rem(self.j // (1 << b), 2)

    def over(self, b):
        step = 2 << b
        return (self.d + step - 2 * step * self.chip_bit(b), self.t)

    def right(self):
        return (self.d, jnp.minimum(self.t + 1, self.nt - 1))

    def left(self):
        return (self.d, jnp.maximum(self.t - 1, 0))


def remote(src, dst, send, recv, device):
    return pltpu.make_async_remote_copy(
        src_ref=src, dst_ref=dst, send_sem=send, recv_sem=recv, device_id=device, device_id_type=MESH
    )


def greet(place, dp_peers):
    barrier = pltpu.get_barrier_semaphore()
    count = 0
    for k in range(1, place.nd if dp_peers == "all" else 1):
        pl.semaphore_signal(
            barrier, inc=1, device_id=(lax.rem(place.d + k, place.nd), place.t), device_id_type=MESH
        )
        count += 1
    if dp_peers == "pair":
        pl.semaphore_signal(barrier, inc=1, device_id=place.pair(), device_id_type=MESH)
        count += 1
    for k in range(1, place.nt):
        pl.semaphore_signal(
            barrier, inc=1, device_id=(place.d, lax.rem(place.t + k, place.nt)), device_id_type=MESH
        )
        count += 1
    pl.semaphore_wait(barrier, count)


BK = 512
TW = 256


def mm(a, b, ca=1, cb=0):
    return lax.dot_general(a, b, (((ca,), (cb,)), ((), ())), preferred_element_type=F32)


def at256(i):
    return pl.ds(pl.multiple_of(i * TW, TW), TW)


class Plan:
    def __init__(self, nd, nt, units, heads, ub):
        self.nd, self.nt = nd, nt
        self.nch = nd // 2
        self.bits = self.nch.bit_length() - 1
        self.units, self.heads, self.ub = units, heads, ub
        self.hw = heads * HD
        self.nu = units // BK
        self.width = nt * BK
        self.rb = self.width // nd
        self.rd = 2 * self.hw // nd
        n = 0
        for name, size in (
            ("xb", 2 * nt),
            ("cb", 2 * nt),
            ("hb", 2 * nt),
            ("w1b", 2 * nt + 1),
            ("w2b", 2 * nt + 1),
            ("f2b", self.nu * nt),
            ("f1b", self.nu * nt),
            ("xo", 1),
            ("co", 1),
        ):
            setattr(self, name, n)
            n += size
        self.blocks = n
        self.n2 = 2 * nt
        self.n1 = 2 * (units // TW)
        self.n3 = 2 * 3
        self.pieces = self.n2 + self.n1 + self.n3 + 2


class Piece:
    def __init__(self, place, order, view, recv, ss, rs):
        self.p, self.order, self.view, self.r, self.ss, self.rs = place, order, view, recv, ss, rs
        self.off = [0]
        for i in range(len(order)):
            self.off.append(self.off[-1] + (place.nch >> (i + 1)))

    def block(self, i, m, mine):
        j = 0
        for b in self.order[:i]:
            j = j + self.p.chip_bit(b) * (1 << b)
        if i < len(self.order):
            b = self.order[i]
            v = self.p.chip_bit(b)
            j = j + (v if mine else 1 - v) * (1 << b)
            for q, b2 in enumerate(self.order[i + 1 :]):
                j = j + ((m >> q) & 1) * (1 << b2)
        return j

    def held(self, i, m, before):
        idx = 0
        for r in range(before + 1, min(i, len(self.order))):
            idx = idx + self.p.chip_bit(self.order[r]) * (1 << (r - before - 1))
        if i < len(self.order):
            v = self.p.chip_bit(self.order[i])
            idx = idx + (1 - v) * (1 << (i - before - 1)) + m * (1 << (i - before))
        return self.off[before] + idx

    def copy(self, i, m):
        k = self.off[i] + m
        return remote(
            self.view(self.block(i, m, False)),
            self.r.at[k],
            self.ss.at[k],
            self.rs.at[k],
            self.p.over(self.order[i]),
        )

    def total(self, i, m):
        acc = self.view(self.block(i, m, False))[...].astype(F32)
        for before in range(i):
            acc = acc + self.r[self.held(i, m, before)].astype(F32)
        return acc

    def start(self, i):
        for m in range(self.p.nch >> (i + 1)):
            if i > 0:
                self.view(self.block(i, m, False))[...] = self.total(i, m).astype(BF16)
            self.copy(i, m).start()

    def wait(self, i):
        for m in range(self.p.nch >> (i + 1)):
            self.copy(i, m).wait()

    def final(self):
        return self.total(len(self.order), 0)


def block_kernel(pn, direct, *refs):
    (
        x_in, c_in, tab_in, segr_in, gain, shift, w1, w2, wq, wd, b1, qvb, kb, obias,
        block_out, input_grad, norm_out, qkv_out, qvb_out, keyb_out, dense_out, fc1_out, fc1b_out,
        fc2_out, outb_out,
        pool, wq_v, wd_v, tab, segr, act, buf, slope, qkv, attn, attn_p, dl, at_tmp, dg, dr, rp, fs, fr,
        ostage, mean_v, inv_v, bias3, fb, ob, ng, sv, rv, stc, stt, sr,
        s_load, s_z, r_z, s_c, r_c, s_tab, s_p, r_p, s_d, r_d, s_f, s_os, s_a, s_oc, r_oc, s_ol, r_ol,
        s_hc, r_hc, s_hl, r_hl, s_v, r_v, s_s, r_s, credit,
    ) = refs
    nd, nt, nch, nu = pn.nd, pn.nt, pn.nch, pn.nu
    hw, ub, rb, rd = pn.hw, pn.ub, pn.rb, pn.rd
    place = Place(nd, nt)
    t, c, d = place.t, place.c, place.d
    nq = pn.units // TW

    def load(i, src, dst):
        return pltpu.make_async_copy(src, dst, s_load.at[i])

    loads = {
        "x": [load(0, x_in, pool.at[pn.xb + t])],
        "c": [load(1, c_in, pool.at[pn.cb + t])],
        "tab": [load(2, tab_in, tab.at[0]), load(3, segr_in, segr.at[0])],
        "wd": [load(4, wd.at[pl.ds(pl.multiple_of(c * hw, hw), hw), :], wd_v)],
        "wq": [
            load(5, wq, wq_v)
        ],
        "xo": [load(8, x_in, pool.at[pn.xo]), load(9, c_in, pool.at[pn.co])],
        "w1": [],
        "w2": [],
        "w1r": [],
    }
    n = 10
    for q in range(nq):
        col = (2 * q + c if direct else q) * TW
        src = w1.at[:, :, pl.ds(pl.multiple_of(col, TW), TW)]
        half = pl.ds((q % 2) * TW, TW)
        loads["w1"].append(load(n, src, pool.at[pl.ds(pn.w1b + (q // 2) * nt, nt), :, half]))
        loads["w1r"].append(load(n + 1, src, pool.at[pl.ds(pn.cb + (q // 2) * nt, nt), :, half]))
        n += 2
        for k in range(nt):
            src = w2.at[pl.ds(pl.multiple_of(col, TW), TW), pl.ds(k * BK, BK)]
            loads["w2"].append(load(n, src, pool.at[pn.w2b + (q // 2) * nt + k, half, :]))
            n += 1

    def begin(*names):
        for name in names:
            for cp in loads[name]:
                cp.start()

    def arrive(*names):
        for name in names:
            for cp in loads[name]:
                cp.wait()

    begin("x", "c", "tab", "w1", "wq", "wd", "w2", "xo")
    greet(place, "all")

    def blk(a, s, k):
        return pool.at[a * (pn.cb - pn.xb) + pn.xb + s * nt + k]

    def z_copy(a, k, side):
        return remote(
            blk(a, 0, k), blk(a, 0, k), s_z.at[side, a, k], r_z.at[a, k],
            place.right() if side == 0 else place.left(),
        )

    def c_copy(a, k):
        return remote(blk(a, 0, k), blk(a, 1, k), s_c.at[a, k], r_c.at[a, k], place.pair())

    def tab_copies():
        return (
            remote(tab.at[0], tab.at[1], s_tab.at[0], s_tab.at[1], place.pair()),
            remote(segr.at[0], segr.at[1], s_tab.at[2], s_tab.at[3], place.pair()),
        )

    def item(side, who, i):
        if side == 0:
            first = i <= who
            return jnp.where(first, 0, 1), jnp.where(first, who - i, 2 * who + 1 - i)
        m = nt - who
        first = i < m
        return jnp.where(first, 0, 1), jnp.where(first, who + i, who + i - m)

    def progress(step):
        if step >= 1:
            @pl.when((t > 0) & (step - 1 < 2 * t))
            def _():
                a, k = item(0, t - 1, step - 1)
                z_copy(a, k, 0).wait_recv()
                c_copy(a, k).start()

            @pl.when((t < nt - 1) & (step - 1 < 2 * (nt - 1 - t)))
            def _():
                a, k = item(1, t + 1, step - 1)
                z_copy(a, k, 1).wait_recv()
                c_copy(a, k).start()

        for side in range(2):
            me = t if side == 0 else nt - 1 - t

            @pl.when((me < nt - 1) & (step <= me))
            def _():
                z_copy(0, me - step if side == 0 else nt - 1 - me + step, side).start()

            @pl.when((me < nt - 1) & (step >= me) & (step <= 2 * me))
            def _():
                k = 2 * me - step
                z_copy(1, k if side == 0 else nt - 1 - k, side).start()

    def z_sent(a):
        for m in range(nt):
            for side in range(2):
                me = t if side == 0 else nt - 1 - t

                @pl.when((me < nt - 1) & (m <= me))
                def _():
                    k = me - m
                    z_copy(a, k if side == 0 else nt - 1 - k, side).wait_send()

        for k in range(nt):
            c_copy(a, k).wait_send()

    def arrival(tt, k):
        if k == tt:
            return -1
        return 2 * tt - 1 - k if k < tt else (nt - 1 - tt) + (k - tt - 1)

    orders = [sorted(range(nt), key=lambda k, tt=tt: (arrival(tt, k), k)) for tt in range(nt)]
    needed = [max(arrival(tt, orders[tt][i]) for tt in range(nt)) + 1 for i in range(nt)]

    def chunk(i):
        k = orders[0][i]
        for tt in range(1, nt):
            k = jnp.where(t == tt, orders[tt][i], k)
        return k

    arrive("x", "c", "tab")
    progress(0)
    c_copy(0, t).start()
    c_copy(1, t).start()
    for cp in tab_copies():
        cp.start()
    fb[...] = jnp.zeros_like(fb)
    bias3[...] = jnp.zeros_like(bias3)
    ng[...] = jnp.zeros_like(ng)
    for step in range(1, nt):
        progress(step)
    for k in range(nt):
        c_copy(0, k).wait_recv()

    lr = 32

    @pl.loop(0, 2 * BK // lr)
    def _(q):
        s = q // (BK // lr)
        rows = pl.ds(pl.multiple_of(lax.rem(q, BK // lr) * lr, lr), lr)
        xs = [pool[pn.xb + s * nt + k, rows, :].astype(F32) for k in range(nt)]
        mean = sum(jnp.sum(v, axis=1, keepdims=True) for v in xs) / pn.width
        xs = [v - mean for v in xs]
        var = sum(jnp.sum(v * v, axis=1, keepdims=True) for v in xs) / pn.width
        inv = lax.rsqrt(var + norm_epsilon)
        for k in range(nt):
            cols = pl.ds(k * BK, BK)
            pool[pn.hb + s * nt + k, rows, :] = (xs[k] * inv * gain[:, cols] + shift[:, cols]).astype(BF16)

        @pl.when(s == 0)
        def _():
            mean_v[rows, :] = jnp.broadcast_to(mean, (lr, LANES))
            inv_v[rows, :] = jnp.broadcast_to(inv, (lr, LANES))

    for cp in tab_copies():
        cp.wait()
    arrive("w1")

    def live(s):
        return tab[s, :, pl.ds(2 * LANES, 1)] >= 0.0

    @pl.loop(0, 2 * nq)
    def _(i):
        s, q = i // nq, lax.rem(i, nq)
        half = at256(lax.rem(q, 2))
        pre = sum(
            mm(pool[pn.hb + s * nt + k], pool[pn.w1b + (q // 2) * nt + k, :, half]) for k in range(nt)
        )
        col = (2 * q + c if direct else q) * TW
        pre = pre + b1[:, pl.ds(pl.multiple_of(col, TW), TW)]
        val, slo = gelu_pair(pre)
        val = val.astype(BF16)
        act[s, :, at256(q)] = val
        slope[s, :, at256(q)] = slo
        val = jnp.where(live(s), val, jnp.zeros_like(val))
        buf[at256(q), pl.ds(pl.multiple_of(s * BK, BK), BK)] = val.T

    def tell(i):
        def signal(n, device):
            pl.semaphore_signal(credit.at[3 * i + n], inc=1, device_id=device, device_id_type=MESH)

        signal(0, place.pair())
        pl.when(t > 0)(lambda: signal(2, place.left()))
        pl.when(t < nt - 1)(lambda: signal(1, place.right()))

    def told(i):
        pl.semaphore_wait(credit.at[3 * i], 1)
        pl.when(t > 0)(lambda: pl.semaphore_wait(credit.at[3 * i + 1], 1))
        pl.when(t < nt - 1)(lambda: pl.semaphore_wait(credit.at[3 * i + 2], 1))

    tell(0)

    orders_ab = [list(range(pn.bits)), list(range(pn.bits))[::-1]]

    def piece(index, half, view, recv):
        return Piece(place, orders_ab[half], view, recv, s_p.at[index], r_p.at[index])

    per2 = BK // ub

    def view2(i, h):
        def view(j):
            return pool.at[
                pn.f2b + nu * i + j // per2,
                pl.ds(pl.multiple_of(lax.rem(j, per2) * ub, ub), ub),
                pl.ds(h * TW, TW),
            ]

        return view

    def view1(q, h):
        def view(j):
            r = 2 * j * rb + h * rb
            return pool.at[
                pn.f1b + nu * (r // BK) + q // 2,
                pl.ds(pl.multiple_of(lax.rem(r, BK), rb), rb),
                pl.ds((q % 2) * TW, TW),
            ]

        return view

    def view3(i, h):
        def view(j):
            r = 2 * j * rb + h * rb
            if i < 2:
                b, col = pn.f2b + r // BK, i * TW
            else:
                b, col = pn.f2b + nt + r // (2 * BK), pl.multiple_of(lax.rem(r // BK, 2) * TW, TW)
            return pool.at[b, pl.ds(pl.multiple_of(lax.rem(r, BK), rb), rb), pl.ds(col, TW)]

        return view

    def view_d(h):
        w = pn.width // 2

        def view(j):
            return dg.at[pl.ds(pl.multiple_of(j * rd, rd), rd), pl.ds(h * w, w)]

        return view

    fc2_p = [[piece(2 * i + h, h, view2(i, h), rp.at[2 * i + h]) for h in range(2)] for i in range(nt)]
    fc1_p = [
        [piece(pn.n2 + 2 * q + h, h, view1(q, h), rp.at[pn.n2 + 2 * q + h]) for h in range(2)]
        for q in range(nq)
    ]
    qkv_p = [
        [piece(pn.n2 + pn.n1 + 2 * i + h, h, view3(i, h), rp.at[2 * i + h]) for h in range(2)]
        for i in range(3)
    ]
    den_p = [piece(pn.n2 + pn.n1 + pn.n3 + h, h, view_d(h), dr.at[h]) for h in range(2)]

    os_used = []

    def stage_out(value_to, dst):
        n = len(os_used)
        slot = n % ostage.shape[0]
        if n >= ostage.shape[0]:
            os_used[n - ostage.shape[0]].wait()
        value_to(ostage.at[slot])
        cp = pltpu.make_async_copy(ostage.at[slot, pl.ds(0, dst.shape[0]), :], dst, s_os.at[slot])
        cp.start()
        os_used.append(cp)

    def fin2(i):
        for h in range(2):
            p = fc2_p[i][h]
            p.wait(pn.bits - 1)

            def put(ref, p=p):
                ref[pl.ds(0, ub), :] = p.final()

            col = chunk(i) * BK + h * TW
            stage_out(put, fc2_out.at[:, pl.ds(pl.multiple_of(col, TW), TW)])

    def send_pair(slot):
        return remote(fs.at[slot], fr.at[slot], s_f.at[0, slot], s_f.at[1, slot], place.pair())

    def fin_pair(pieces, slot, dst):
        for h in range(2):
            pieces[h].wait(pn.bits - 1)

        def put(ref):
            for h in range(2):
                @pl.when(c == h)
                def _():
                    ref[pl.ds(0, rb), :] = pieces[h].final()

                @pl.when(c != h)
                def _():
                    fs[slot] = pieces[h].final().astype(BF16)

        stage_out(put, dst)
        send_pair(slot).start()

    def dst1(q, core):
        col = (2 * q + core) * TW if direct else core * pn.units + q * TW
        return fc1_out.at[:, pl.ds(pl.multiple_of(col, TW), TW)]

    def dst3(i, core):
        return qkv_out.at[i, :, pl.ds(pl.multiple_of(core * hw, hw), hw)]

    def fin1(q):
        fin_pair(fc1_p[q], q, dst1(q, c))

    def fin3(i):
        fin_pair(qkv_p[i], nq + i, dst3(i, c))

    def fin_d():
        for h in range(2):
            den_p[h].wait(pn.bits - 1)
            for w in range(pn.width // 2 // TW):

                def put(ref, h=h, w=w):
                    p = den_p[h]
                    cols = pl.ds(w * TW, TW)
                    blk_me = p.block(len(p.order), 0, True)
                    acc = dg[pl.ds(pl.multiple_of(blk_me * rd, rd), rd), pl.ds(h * (pn.width // 2) + w * TW, TW)].astype(F32)
                    for before in range(len(p.order)):
                        acc = acc + p.r[p.held(len(p.order), 0, before), :, cols].astype(F32)
                    ref[pl.ds(0, rd), :] = acc

                stage_out(put, dense_out.at[:, pl.ds(h * (pn.width // 2) + w * TW, TW)])

    def mids(pieces, i):
        for p in pieces:
            p.wait(i - 1)
            p.start(i)

    def mid(pieces):
        for i in range(1, pn.bits):
            mids(pieces, i)

    def fc2_chunk(i):
        k = chunk(i)
        c_copy(1, k).wait_recv()

        @pl.loop(0, 2 * nu)
        def _(q):
            u, h = q // 2, lax.rem(q, 2)
            rows = pl.ds(pl.multiple_of(u * BK, BK), BK)
            out = mm(buf[rows, pl.ds(0, BK)], pool[pn.cb + k, :, at256(h)]) + mm(
                buf[rows, pl.ds(BK, BK)], pool[pn.cb + nt + k, :, at256(h)]
            )
            pool[pn.f2b + nu * i + u, :, at256(h)] = out.astype(BF16)

        for p in fc2_p[i]:
            p.start(0)

    done_steps = [nt - 1]

    def upto(step):
        while done_steps[0] < min(step, 2 * nt - 2):
            done_steps[0] += 1
            progress(done_steps[0])

    fc2_chunk(0)
    upto(needed[1])
    fc2_chunk(1)

    arrive("wq")
    lane = lax.broadcasted_iota(jnp.int32, (BK, TW), 1)
    low = lax.rem(lane, ROT) < ROT // 2

    def swap(v):
        return jnp.where(low, pltpu.roll(v, TW - ROT // 2, 1), pltpu.roll(v, ROT // 2, 1))

    def table(s, i):
        v = tab[s, :, pl.ds(i * LANES, LANES)]
        return jnp.concatenate([v, v], axis=1)

    @pl.loop(0, 2)
    def _(s):
        for i in range(3):
            v = sum(mm(pool[pn.hb + s * nt + k], wq_v[i, pl.ds(k * BK, BK), :]) for k in range(nt))
            cols = pl.ds(pl.multiple_of(c * hw, hw), hw)
            if i == 1:
                v = v + kb[:, cols]
            else:
                v = v + qvb[pl.ds(i // 2, 1), cols]
            if i < 2:
                v = v * table(s, 0) + swap(v) * table(s, 1)
            qkv[i, s] = v.astype(BF16)

    mid(fc2_p[0])
    z_sent(0)

    @pl.loop(0, 2 * nt)
    def _(i):
        for h in range(2):
            pool[pn.xb + i, :, pl.ds(h * TW, TW)] = pool[pn.hb + i, pl.ds(h * TW, TW), :].T

    upto(needed[2])
    fc2_chunk(2)
    mid(fc2_p[1])

    lane1 = lax.broadcasted_iota(jnp.int32, (1, LANES), 1)
    heads2 = [lane1 < HD, lane1 >= HD]
    score_scale = HD ** (-0.5)

    def only(v, h):
        return jnp.where(heads2[h], v, jnp.zeros_like(v))

    def bias_of(s, qt):
        nk = (qt + 1) * TW
        col = lax.broadcasted_iota(jnp.int32, (TW, nk), 1)
        row = lax.broadcasted_iota(jnp.int32, (TW, nk), 0) + qt * TW
        same = tab[s, pl.ds(qt * TW, TW), pl.ds(2 * LANES, 1)] == segr[s, pl.ds(0, 1), pl.ds(0, nk)]
        return jnp.where(same & (col <= row), 0.0, masked_score)

    def probs(qh, keys, bias):
        sc = mm(qh, keys, 1, 1) * score_scale + bias
        top = jnp.max(sc, axis=1, keepdims=True)
        ex = jnp.exp(sc - top)
        return ex * (1.0 / jnp.sum(ex, axis=1, keepdims=True))

    npair = hw // LANES

    @pl.loop(0, 2 * npair)
    def _(i):
        s, hp = i // npair, lax.rem(i, npair)
        cols = pl.ds(pl.multiple_of(hp * LANES, LANES), LANES)
        for qt in range(2):
            rows, kr = pl.ds(qt * TW, TW), pl.ds(0, (qt + 1) * TW)
            bias = bias_of(s, qt)
            out = []
            for h in range(2):
                pb = probs(only(qkv[0, s, rows, cols], h), qkv[1, s, kr, cols], bias).astype(BF16)
                out.append(mm(pb, qkv[2, s, kr, cols]))
            attn[s, rows, cols] = jnp.where(heads2[0], out[0], out[1]).astype(BF16)

    def attn_copy(s):
        return remote(attn.at[s], attn_p.at[1 - s], s_a.at[0, s], s_a.at[1, s], place.pair())

    attn_copy(0).start()
    attn_copy(1).start()
    arrive("wd", "w2")

    @pl.loop(0, 2 * nt * 2)
    def _(i):
        b, h = i // 2, lax.rem(i, 2)
        s, k = b // nt, lax.rem(b, nt)
        half = at256(h)
        out = mm(attn[s], wd_v[:, pl.ds(pl.multiple_of(k * BK + h * TW, TW), TW)])
        for u in range(nu):
            out = out + mm(act[s, :, pl.ds(u * BK, BK)], pool[pn.w2b + u * nt + k, :, half])
        pool[pn.hb + b, :, half] = out.astype(BF16)

    class Line:
        def __init__(self, pr, rbase, sp, rp_, sl, rl):
            self.pr, self.rbase, self.sp, self.rp, self.sl, self.rl = pr, rbase, sp, rp_, sl, rl

        def pair(self, k):
            return remote(
                pool.at[pn.hb + nt + k], pool.at[self.pr + k], self.sp.at[k], self.rp.at[k], place.pair()
            )

        def copy(self, side, k, dev):
            if side == 0:
                slot = k
            else:
                slot = jnp.where(k == t - 1, nt, k)
            return remote(
                pool.at[pn.hb + k], pool.at[self.rbase + slot], self.sl.at[side, k], self.rl.at[slot], dev
            )

        def got(self, slot):
            remote(
                pool.at[pn.hb], pool.at[self.rbase + slot], self.sl.at[0, 0], self.rl.at[slot], place.pair()
            ).wait_recv()

        def send(self, side, step):
            me = t if side == 0 else nt - 1 - t

            @pl.when((me <= step) & (me < nt - 1))
            def _():
                k = nt - 1 - step + me
                k = k if side == 0 else nt - 1 - k

                @pl.when(me > 0)
                def _():
                    self.got(k)

                @pl.loop(0, BK // 64)
                def _(q):
                    rows = pl.ds(pl.multiple_of(q * 64, 64), 64)
                    v = pool[pn.hb + k, rows, :].astype(F32) + pool[self.pr + k, rows, :].astype(F32)
                    r = pool[self.rbase + k, rows, :].astype(F32)
                    pool[pn.hb + k, rows, :] = (v + jnp.where(me > 0, r, 0.0)).astype(BF16)

                self.copy(side, k, place.right() if side == 0 else place.left()).start()

        def sent(self):
            for side in range(2):
                me = t if side == 0 else nt - 1 - t
                for step in range(nt - 1):
                    @pl.when((me <= step) & (me < nt - 1))
                    def _():
                        k = nt - 1 - step + me
                        k = k if side == 0 else nt - 1 - k
                        self.copy(side, k, place.pair()).wait_send()

        def finish(self):
            @pl.when(t > 0)
            def _():
                self.got(t)

            @pl.when(t < nt - 1)
            def _():
                self.got(nt)

        def value(self, rows):
            v = pool[pn.hb + t, rows, :].astype(F32) + pool[self.pr + t, rows, :].astype(F32)
            v = v + jnp.where(t > 0, pool[self.rbase + t, rows, :].astype(F32), 0.0)
            return v + jnp.where(t < nt - 1, pool[self.rbase + nt, rows, :].astype(F32), 0.0)

    line_o = Line(pn.w1b, pn.w1b + nt, s_oc, r_oc, s_ol, r_ol)
    line_h = Line(pn.w2b, pn.w2b + nt, s_hc, r_hc, s_hl, r_hl)
    told(0)
    for k in range(nt):
        line_o.pair(k).start()

    upto(needed[3])
    fc2_chunk(3) if nt > 3 else None
    mid(fc2_p[2])

    @pl.loop(0, 2 * nq)
    def _(i):
        s, q = i // nq, lax.rem(i, nq)
        rows = at256(lax.rem(q, 2))
        v = sum(
            mm(pool[pn.cb + s * nt + k], pool[pn.w2b + (q // 2) * nt + k, rows, :], 1, 1) for k in range(nt)
        )
        v = jnp.where(live(s), v * slope[s, :, at256(q)], 0.0)
        act[s, :, at256(q)] = v.astype(BF16)
        fb[pl.ds(0, 1), at256(q)] += jnp.sum(v, axis=0, keepdims=True)

    tell(1)
    for k in range(nt):
        line_o.pair(k).wait()
    line_o.send(0, 0)
    line_o.send(1, 0)

    def fc1_chunk(q):
        @pl.loop(0, nt)
        def _(k):
            cols = pl.ds(q * TW, TW)
            out = mm(pool[pn.xb + k], act[0, :, cols]) + mm(pool[pn.xb + nt + k], act[1, :, cols])
            pool[pn.f1b + nu * k + q // 2, :, pl.ds((q % 2) * TW, TW)] = out.astype(BF16)

        for p in fc1_p[q]:
            p.start(0)

    fc1_chunk(0)
    mid(fc2_p[3])
    fc1_chunk(1)
    fin2(0)
    fin2(1)
    line_o.send(0, 1)
    line_o.send(1, 1)

    def dcols(i):
        return pl.ds(i * hw, hw)

    @pl.loop(0, 2)
    def _(s):
        v = sum(mm(pool[pn.cb + s * nt + k], wd_v[:, pl.ds(k * BK, BK)], 1, 1) for k in range(nt))
        v = jnp.where(live(s), v, 0.0)
        buf[pl.ds(pl.multiple_of(s * BK, BK), BK), dcols(3)] = v.astype(BF16)

    ob[...] = jnp.broadcast_to(
        jnp.sum(jnp.where(live(0), pool[pn.cb + t].astype(F32), 0.0), axis=0, keepdims=True), ob.shape
    )
    for s in range(2):
        attn_copy(s).wait()
    for core in range(2):
        for s in range(2):
            mine = attn if core == 0 else attn_p
            v = jnp.where(live(s), mine[s], jnp.zeros((BK, hw), BF16))
            at_tmp[...] = v.T
            who = c if core == 0 else 1 - c
            for j in range(nch // 2):
                off = lax.rem((2 * j + c) * rd, hw)
                dst = (who * (nch // 2) + j) * rd
                dl[pl.ds(pl.multiple_of(dst, rd), rd), pl.ds(s * BK, BK)] = at_tmp[
                    pl.ds(pl.multiple_of(off, rd), rd), :
                ]

    @pl.loop(0, 2 * nt)
    def _(i):
        k, h = i // 2, lax.rem(i, 2)
        out = mm(dl[:, pl.ds(0, BK)], pool[pn.cb + k, :, at256(h)]) + mm(
            dl[:, pl.ds(BK, BK)], pool[pn.cb + nt + k, :, at256(h)]
        )
        dg[:, pl.ds(pl.multiple_of(i * TW, TW), TW)] = out.astype(BF16)

    z_sent(1)
    begin("w1r")
    fc1_chunk(2)
    mid(fc1_p[0])
    fin2(2)
    fc1_chunk(3) if nq > 3 else None
    mid(fc1_p[1])
    for p in den_p:
        p.start(0)
    fin2(3) if nt > 3 else None
    for b in range(pn.bits):
        pl.semaphore_signal(credit.at[6 + b], inc=1, device_id=place.over(b), device_id_type=MESH)
    line_o.send(0, 2) if nt > 3 else None
    line_o.send(1, 2) if nt > 3 else None

    @pl.loop(0, 2 * npair)
    def _(i):
        s, hp = i // npair, lax.rem(i, npair)
        cols = pl.ds(pl.multiple_of(hp * LANES, LANES), LANES)
        base = pl.multiple_of(s * BK, BK)
        dq, dk, dv = [], [None, None], [None, None]
        for qt in range(2):
            rows, kr, nk = pl.ds(qt * TW, TW), pl.ds(0, (qt + 1) * TW), (qt + 1) * TW
            bias = bias_of(s, qt)
            da = buf[pl.ds(base + qt * TW, TW), pl.ds(pl.multiple_of(3 * hw + hp * LANES, LANES), LANES)]
            prod = da.astype(F32) * attn[s, rows, cols].astype(F32)
            qs, ks, vs = qkv[0, s, rows, cols], qkv[1, s, kr, cols], qkv[2, s, kr, cols]
            got = []
            for h in range(2):
                pf = probs(only(qs, h), ks, bias)
                pb = pf.astype(BF16)
                delta = jnp.sum(only(prod, h), axis=1, keepdims=True)
                dp = mm(only(da, h), vs, 1, 1)
                ds = (pf * (dp - delta) * score_scale).astype(BF16)
                got.append((mm(ds, ks), mm(ds, qs, 0, 0), mm(pb, da, 0, 0)))
            pick = [jnp.where(heads2[0], a, b) for a, b in zip(*got)]
            dq.append(pick[0])
            for lst, v in ((dk, pick[1]), (dv, pick[2])):
                lst[0] = v[:TW] if lst[0] is None else lst[0] + v[:TW]
                if qt:
                    lst[1] = v[TW:]
        low1 = lax.rem(lane1, ROT) < ROT // 2
        for i3, parts in enumerate((dq, dk, dv)):
            for qt in range(2):
                rows = pl.ds(qt * TW, TW)
                v = parts[qt]
                if i3 < 2:
                    sw = jnp.where(
                        low1, pltpu.roll(v, LANES - ROT // 2, 1), pltpu.roll(v, ROT // 2, 1)
                    )
                    v = v * tab[s, rows, pl.ds(0, LANES)] - sw * tab[s, rows, pl.ds(LANES, LANES)]
                bias3[i3, pl.ds(0, 1), cols] += jnp.sum(v, axis=0, keepdims=True)
                buf[
                    pl.ds(base + qt * TW, TW), pl.ds(pl.multiple_of(i3 * hw + hp * LANES, LANES), LANES)
                ] = v.astype(BF16)

    mid(fc1_p[2])
    mid(den_p)
    for b in range(pn.bits):
        pl.semaphore_wait(credit.at[6 + b], 1)

    def qkv_chunk(i):
        @pl.loop(0, nt)
        def _(k):
            out = mm(pool[pn.xb + k], buf[pl.ds(0, BK), dcols(i)]) + mm(
                pool[pn.xb + nt + k], buf[pl.ds(BK, BK), dcols(i)]
            )
            if i < 2:
                pool[pn.f2b + k, :, pl.ds(i * TW, TW)] = out.astype(BF16)
            else:
                pool[pn.f2b + nt + k // 2, :, at256(lax.rem(k, 2))] = out.astype(BF16)

        for p in qkv_p[i]:
            p.start(0)

    qkv_chunk(0)
    mid(fc1_p[3]) if nq > 3 else None
    fin1(0)
    qkv_chunk(1)
    fin1(1)
    qkv_chunk(2)

    arrive("xo")
    line_o.finish()

    @pl.loop(0, BK // 64)
    def _(q):
        rows = pl.ds(pl.multiple_of(q * 64, 64), 64)
        ocol = pl.ds(pl.multiple_of(t * BK, BK), BK)
        v = pool[pn.xo, rows, :].astype(F32) + line_o.value(rows)
        v = v + (obias[pl.ds(0, 1), ocol] + obias[pl.ds(1, 1), ocol])
        block_out[rows, :] = v.astype(BF16)

    line_o.sent()

    arrive("w1r")

    def dh_chunk(b):
        s, k = b // nt, lax.rem(b, nt)

        @pl.loop(0, 2)
        def _(h):
            rows = at256(h)
            base = pl.multiple_of(s * BK, BK)
            out = 0.0
            for i in range(3):
                out = out + mm(
                    buf[pl.ds(base, BK), dcols(i)],
                    wq_v[i, pl.ds(pl.multiple_of(k * BK + h * TW, TW), TW), :], 1, 1,
                )
            for u in range(nu):
                out = out + mm(act[s, :, pl.ds(u * BK, BK)], pool[pn.cb + u * nt + k, rows, :], 1, 1)
            pool[pn.hb + b, :, rows] = out.astype(BF16)

    told(1)

    @pl.loop(0, nt)
    def _(k):
        dh_chunk(nt + k)
        line_h.pair(k).start()

    mid(qkv_p[0])
    fin1(2)

    @pl.loop(0, nt)
    def _(k):
        dh_chunk(k)

    for k in range(nt):
        line_h.pair(k).wait()
    line_h.send(0, 0)
    line_h.send(1, 0)
    fin1(3) if nq > 3 else None
    fin_d()
    mid(qkv_p[1])
    line_h.send(0, 1)
    line_h.send(1, 1)
    mid(qkv_p[2])
    fin3(0)
    if nt > 3:
        line_h.send(0, 2)
        line_h.send(1, 2)
    fin3(1)

    line_h.finish()
    gcol = pl.ds(pl.multiple_of(t * BK, BK), BK)

    def tail(rows):
        dh = line_h.value(rows)
        normed = (pool[pn.xo, rows, :].astype(F32) - mean_v[rows, pl.ds(0, 1)]) * inv_v[rows, pl.ds(0, 1)]
        return dh, normed, dh * gain[:, gcol]

    first = lax.broadcasted_iota(jnp.int32, (64, LANES), 1) == 0

    @pl.loop(0, BK // 64)
    def _(q):
        rows = pl.ds(pl.multiple_of(q * 64, 64), 64)
        dh, normed, scaled = tail(rows)
        s1 = jnp.sum(scaled, axis=1, keepdims=True)
        s2 = jnp.sum(scaled * normed, axis=1, keepdims=True)
        stc[rows, :] = jnp.where(first, s1, s2)
        ng[pl.ds(0, 1), :] += jnp.sum(dh * normed, axis=0, keepdims=True)
        ng[pl.ds(1, 1), :] += jnp.sum(dh, axis=0, keepdims=True)

    stt[...] = stc[...].T[:8]

    def s_copy(k):
        return remote(stt, sr.at[t], s_s.at[k], r_s.at[t], (d, lax.rem(t + k, nt)))

    def v_copy(k):
        peer = lax.rem(d + k, nd)
        return remote(sv.at[peer], rv.at[d], s_v.at[k], r_v.at[d], (peer, t))

    for k in range(1, nt):
        s_copy(k).start()
    cw, hwd = BK // nd, 2 * hw // nd
    sv[...] = jnp.zeros_like(sv)
    for dd in range(nd):
        mine = c == dd % 2
        sv[dd, pl.ds(0, 1), pl.ds(0, ub)] = jnp.where(mine, fb[pl.ds(0, 1), pl.ds((dd // 2) * ub, ub)], 0.0)
        sv[dd, pl.ds(1, 2), pl.ds(0, cw)] = ng[pl.ds(0, 2), pl.ds(dd * cw, cw)]
        sv[dd, pl.ds(3, 1), pl.ds(0, cw)] = ob[pl.ds(0, 1), pl.ds(dd * cw, cw)]
        here = c == (dd * hwd) // hw
        src = pl.ds((dd * hwd) % hw, hwd)
        sv[dd, pl.ds(4, 1), pl.ds(0, hwd)] = jnp.where(here, bias3[0, pl.ds(0, 1), src], 0.0)
        sv[dd, pl.ds(5, 1), pl.ds(0, hwd)] = jnp.where(here, bias3[2, pl.ds(0, 1), src], 0.0)
        for core in range(2):
            sv[dd, pl.ds(6 + core, 1), :] = jnp.where(c == core, bias3[1, pl.ds(0, 1), :], 0.0)
    for k in range(1, nd):
        v_copy(k).start()
    rv[d] = sv[d]
    sr[t] = stt[...]
    fin3(2)
    for slot in range(nq + 3):
        send_pair(slot).wait()

        def put(ref, slot=slot):
            ref[pl.ds(0, rb), :] = fr[slot].astype(F32)

        stage_out(put, dst1(slot, 1 - c) if slot < nq else dst3(slot - nq, 1 - c))
    for k in range(1, nt):
        s_copy(k).wait_send()
        frm = lax.rem(t + k, nt)
        remote(stt, sr.at[frm], s_s.at[k], r_s.at[frm], place.pair()).wait_recv()
    tot = sr[0]
    for k in range(1, nt):
        tot = tot + sr[k]
    stc[...] = jnp.concatenate([tot / pn.width, jnp.zeros((LANES - 8, BK), F32)], axis=0).T

    @pl.loop(0, BK // 64)
    def _(q):
        rows = pl.ds(pl.multiple_of(q * 64, 64), 64)
        dh, normed, scaled = tail(rows)
        v = inv_v[rows, pl.ds(0, 1)] * (scaled - stc[rows, pl.ds(0, 1)] - normed * stc[rows, pl.ds(1, 1)])
        keep = tab[0, rows, pl.ds(2 * LANES, 1)] >= 0.0
        input_grad[rows, :] = v + jnp.where(keep, pool[pn.co, rows, :].astype(F32), 0.0)

    line_h.sent()
    for k in range(1, nd):
        v_copy(k).wait_send()
        frm = lax.rem(d + k, nd)
        remote(sv.at[0], rv.at[frm], s_v.at[k], r_v.at[frm], place.pair()).wait_recv()
    res = rv[0]
    for k in range(1, nd):
        res = res + rv[k]
    fc1b_out[...] = res[0:1, :ub]
    norm_out[...] = res[1:3, :cw]
    outb_out[...] = jnp.concatenate([res[3:4, :cw], res[3:4, :cw]], axis=0)
    qvb_out[...] = res[4:6, :hwd]
    rk = ROT // nd
    turned = pltpu.roll(res, lax.rem(TW - d * rk, TW), 1)
    for core in range(2):
        for h in range(pn.heads):
            keyb_out[pl.ds(core * pn.heads + h, 1), :] = turned[6 + core : 7 + core, h * HD : h * HD + rk]
    for cp in os_used[-ostage.shape[0] :]:
        cp.wait()

def per_device(
    hidden_in,
    cotangent,
    segment_ids,
    positions,
    norm_gain,
    norm_shift,
    qkv_weight,
    qv_bias,
    key_bias,
    dense_weight,
    fc1_weight,
    fc1_bias,
    fc2_weight,
    out_bias,
):
    nd, nt = lax.axis_size("dp"), lax.axis_size("tensor")
    c = lax.rem(lax.axis_index("dp"), 2)
    nch = nd // 2
    rows, wl = hidden_in.shape
    width = wl * nt
    heads = key_bias.shape[0] // 2
    units = fc1_weight.shape[1] // 2
    ub = units // nch
    pn = Plan(nd, nt, units, heads, ub)
    hw, rb, rd, nq = pn.hw, pn.rb, pn.rd, units // TW
    assert rows == BK and wl == BK and nt == 4 and nq == 4 and hw == TW and rb == ub
    direct = ub == TW

    half = ROT // 2
    lane = jnp.arange(LANES, dtype=jnp.int32) % HD
    rotary = lane < ROT
    inverse = jnp.power(jnp.float32(10000.0), -((lane % half).astype(F32) * (2.0 / ROT)))
    angles = positions.astype(F32)[:, None] * inverse[None, :]
    sign = jnp.where(lane < half, -1.0, 1.0)
    seg = segment_ids.astype(F32)
    tab = jnp.concatenate(
        [
            jnp.where(rotary, jnp.cos(angles), 1.0),
            jnp.where(rotary, jnp.sin(angles) * sign, 0.0),
            jnp.broadcast_to(seg[:, None], (rows, LANES)),
        ],
        axis=1,
    )
    segr = jnp.broadcast_to(seg[None, :], (8, rows))
    kb = jnp.concatenate([key_bias, jnp.zeros((2 * heads, HD - ROT), F32)], axis=1).reshape(1, 2 * hw)

    def pick(w, axis):
        shape = w.shape
        w = w.reshape(*shape[:axis], nch, 2, ub, *shape[axis + 1 :])
        w = lax.dynamic_index_in_dim(w, c, axis + 1, keepdims=False)
        return w.reshape(*shape[:axis], units, *shape[axis + 1 :])

    w1, w2, b1 = fc1_weight, fc2_weight, fc1_bias
    if not direct:
        w1, w2, b1 = pick(w1, 1), pick(w2, 0), pick(b1, 0)
    w1 = w1.reshape(nt, BK, w1.shape[1])
    wq = lax.dynamic_slice_in_dim(qkv_weight, c * hw, hw, 2).transpose(1, 0, 2)
    b1 = b1.reshape(1, -1)

    vm = pl.BlockSpec(memory_space=pltpu.VMEM)
    anyw = pl.BlockSpec(memory_space=pl.ANY)
    shapes = [
        ((rows, wl), BF16, vm),
        ((rows, wl), F32, vm),
        ((2, wl // nd), F32, vm),
        ((3, rb, 2 * hw), F32, anyw),
        ((2, 2 * hw // nd), F32, vm),
        ((2 * heads, ROT // nd), F32, vm),
        ((rd, width), F32, anyw),
        ((rb, 2 * units), F32, anyw),
        ((1, ub), F32, vm),
        ((ub, width), F32, anyw),
        ((2, wl // nd), F32, vm),
    ]
    dma = pltpu.SemaphoreType.DMA
    nos = 4
    scratch = [
        pltpu.VMEM((pn.blocks, BK, BK), BF16),
        pltpu.VMEM((3, width, hw), BF16),
        pltpu.VMEM((hw, width), BF16),
        pltpu.VMEM((2, rows, 3 * LANES), F32),
        pltpu.VMEM((2, 8, rows), F32),
        pltpu.VMEM((2, rows, units), BF16),
        pltpu.VMEM((units, 2 * rows), BF16),
        pltpu.VMEM((2, rows, units), F32),
        pltpu.VMEM((3, 2, rows, hw), BF16),
        pltpu.VMEM((2, rows, hw), BF16),
        pltpu.VMEM((2, rows, hw), BF16),
        pltpu.VMEM((nch * rd, 2 * rows), BF16),
        pltpu.VMEM((hw, rows), BF16),
        pltpu.VMEM((nch * rd, width), BF16),
        pltpu.VMEM((2, nch - 1, rd, width // 2), BF16),
        pltpu.VMEM((pn.n2 + pn.n1, nch - 1, rb, TW), BF16),
        pltpu.VMEM((nq + 3, rb, TW), BF16),
        pltpu.VMEM((nq + 3, rb, TW), BF16),
        pltpu.VMEM((nos, max(rb, rd), TW), F32),
        pltpu.VMEM((rows, LANES), F32),
        pltpu.VMEM((rows, LANES), F32),
        pltpu.VMEM((3, 8, hw), F32),
        pltpu.VMEM((8, units), F32),
        pltpu.VMEM((8, wl), F32),
        pltpu.VMEM((8, wl), F32),
        pltpu.VMEM((nd, 8, TW), F32),
        pltpu.VMEM((nd, 8, TW), F32),
        pltpu.VMEM((rows, LANES), F32),
        pltpu.VMEM((8, rows), F32),
        pltpu.VMEM((nt, 8, rows), F32),
        dma((10 + nq * (2 + nt),)),
        dma((2, 2, nt)),
        dma((2, nt)),
        dma((2, nt)),
        dma((2, nt)),
        dma((4,)),
        dma((pn.pieces, nch - 1)),
        dma((pn.pieces, nch - 1)),
        dma((2,)),
        dma((2,)),
        dma((2, nq + 3)),
        dma((nos,)),
        dma((2, 2)),
        dma((nt,)),
        dma((nt,)),
        dma((2, nt)),
        dma((nt + 1,)),
        dma((nt,)),
        dma((nt,)),
        dma((2, nt)),
        dma((nt + 1,)),
        dma((nd,)),
        dma((nd,)),
        dma((nt,)),
        dma((nt,)),
        pltpu.SemaphoreType.REGULAR((6 + pn.bits,)),
    ]
    res = pl.pallas_call(
        functools.partial(block_kernel, pn, direct),
        out_shape=[jax.ShapeDtypeStruct(s, dt) for s, dt, _ in shapes],
        in_specs=[anyw, anyw, anyw, anyw, vm, vm, anyw, anyw, anyw, anyw, vm, vm, vm, vm],
        out_specs=[sp for _, _, sp in shapes],
        scratch_shapes=scratch,
        compiler_params=pltpu.CompilerParams(
            collective_id=0, has_side_effects=True, vmem_limit_bytes=VMEM_BYTES
        ),
        name="block",
    )(
        hidden_in, cotangent, tab, segr, norm_gain.reshape(1, width), norm_shift.reshape(1, width),
        w1, w2, wq, dense_weight, b1, qv_bias, kb, out_bias,
    )
    res = list(res)
    res[3] = res[3].transpose(1, 0, 2)
    if not direct:
        res[7] = res[7].reshape(rb, 2, nch, ub).transpose(0, 2, 1, 3).reshape(rb, 2 * units)
    res[8] = res[8].reshape(ub)
    return tuple(res)


def solution(mesh):
    placed = (
        P("dp", "tensor"),
        P("dp", "tensor"),
        P("dp"),
        P("dp"),
        P(),
        P(),
        P(None, None, "tensor"),
        P(None, "tensor"),
        P("tensor", None),
        P("tensor", None),
        P(None, "tensor"),
        P("tensor"),
        P("tensor", None),
        P(),
    )
    return jax.shard_map(
        per_device,
        mesh=mesh,
        in_specs=placed,
        out_specs=(
            P("dp", "tensor"),
            P("dp", "tensor"),
            P(None, ("tensor", "dp")),
            P("dp", None, "tensor"),
            P(None, ("tensor", "dp")),
            P("tensor", "dp"),
            P(("tensor", "dp"), None),
            P("dp", "tensor"),
            P(("tensor", "dp")),
            P(("tensor", "dp"), None),
            P(None, ("tensor", "dp")),
        ),
        check_vma=False,
    )
```

time: 644 us -> 235 us (0.36)
  waiting for transfers between devices: 424 us -> 0 us
  Pallas kernels: 0 us -> 212 us
  matrix products: 116 us -> 0 us
  other arithmetic: 34.8 us -> 3.33 us
  blocking collectives: 24.4 us -> 0 us
  between operations: 16.2 us -> 0.72 us
    reduce_scatter x4 -> x0, waiting for transfers between devices: 248 us -> none  [the longest x1 72.5 us: per_device(): lax.psum_scatter(fc1_g.astype(jnp.bfloat16), 'dp', scatter_dimension=0, t...]
    pallas_call x0 -> x1, Pallas kernels: none -> 212 us  [per_device(): pl.pallas_call(functools.partial(block_kernel, pn, direct), out_shape=[ja...]
    dot_general x18 -> x0, matrix products: 116 us -> none  [the longest x1 15.1 us: backward_block(): jnp.einsum('qhd,khd->hqk', d_attn, values_b, preferred_element_type=jnp.f...]
    psum x1 -> x0, waiting for transfers between devices: 80.3 us -> none  [per_device(): lax.psum(dh_part.astype(jnp.bfloat16), 'tensor').astype(jnp.float32)]
    all_gather x2 -> x0, waiting for transfers between devices: 74.2 us -> none  [the longest x1 45.1 us: per_device(): lax.all_gather(hidden_in, 'tensor', axis=1, tiled=True)]
    unnamed x1 -> x0, blocking collectives: 24.4 us -> none
    unnamed x13 -> x0, waiting for transfers between devices: 21.4 us -> none
    reduce_sum x9 -> x0, other arithmetic: 15.5 us -> none  [the longest x1 3.66 us: per_device(): jnp.mean(scaled, axis=1, keepdims=True)]
  transfers between devices with their start and end apart: 11 -> 0, of which waited for: 8 -> 0; matrix products, arithmetic and copies ran while one was open for 14% -> 0% of each run, Pallas kernels for 0% -> 0%
where the time goes in v1:
time: 235 us
  Pallas kernels  212 us (90%)
  local copies, waits for them, and re-layouts  18.7 us (8%)
  other arithmetic  3.33 us (1%)
    pallas_call x1, Pallas kernels, per_device(): pl.pallas_call(functools.partial(block_kernel, pn, direct), out_shape=[ja...  212 us
    unnamed x27, local copies, waits for them, and re-layouts  12.9 us

profile of v1, /device:TPU:0, one launch (start us, length us, event | category | flops | bytes accessed | tf_op | source)
XLA Modules:
  0.0 235.0 jit_solution(17124382154453530822)
XLA Ops:
  0.7 0.7 convert_element_type.15
  1.4 0.7 convert_element_type.13
  2.0 0.7 concatenate.7
  2.7 0.7 reshape.75.refs_12_
  3.4 0.6 broadcast_in_dim.44.refs_3_
  4.0 0.1 broadcast_in_dim.43
  4.1 1.0 fusion
  5.2 0.9 pad_maximum_fusion.refs_2_
  6.1 3.7 %dynamic-slice_bitcast_fusion.refs_8_ = bf16[3,2048,256]{2,1,0:T(8,128)(2,1)} fusion(bf16[2048,3,512]{2,0,1:T(8,128)(2,1)} %param.20, s32[]{:T(128)S(6)} %select_n.51), kind=kLoop, calls=%fused_computation | loop fusion | bytes 6291460 | tf_op jit(solution)/shard_map/transpose | solution.py:1093
  9.8 212.2 %block.1 = (bf16[512,512]{1,0:T(8,128)(2,1)}, f32[512,512]{1,0:T(8,128)}, f32[2,64]{1,0:T(2,128)}, f32[3,256,512]{2,1,0:T(8,128)}, f32[2,64]{1,0:T(2,128)}, /*in...) custom-call(bf16[512,512]{1,0:T(8,128)(2,1)} %refs_0_.1, ...), custom_call_target="tpu_custom_call" | custom-call | tf_op jit(solution)/shard_map/block/pallas_call | solution.py:1171
  222.1 1.4 copy.25
  223.5 1.9 copy.36
  225.4 2.3 copy.37
  227.7 0.6 copy.38
  228.2 1.1 copy.39
  229.4 0.0 copy-done.6
  229.4 0.6 copy.40
  229.9 0.0 copy-done.3
  229.9 0.8 copy.41
  230.7 1.3 copy.42
  232.1 0.6 copy.43
  232.6 0.5 copy-done
  233.1 1.3 copy.44
  234.4 0.6 copy.45
  (15 shorter events, 0.0 us)
Async XLA Ops:
  222.1 5.6 %copy-start.7 = (f32[2,64]{1,0:T(2,128)S(1)}, f32[2,64]{1,0:T(2,128)}, u32[]{:S(2)}) copy-start(f32[2,64]{1,0:T(2,128)} %get-tuple-element.61) | copy-start | bytes 1540
  222.1 6.2 %copy-start.2 = (f32[3,256,512]{2,1,0:T(8,128)S(1)}, f32[3,256,512]{2,1,0:T(8,128)}, u32[]{:S(2)}) copy-start(f32[3,256,512]{2,1,0:T(8,128)} %get-tuple-element.25) | copy-start | bytes 4718596
  227.7 1.7 copy-start.6
  227.7 2.3 copy-start.3
  228.2 2.5 %copy-start.1 = (f32[256,2048]{1,0:T(8,128)S(1)}, f32[256,2048]{1,0:T(8,128)}, u32[]{:S(2)}) copy-start(f32[256,2048]{1,0:T(8,128)} %get-tuple-element.66) | copy-start | bytes 6291460
  230.7 1.3 copy-start.5
  230.7 2.4 %copy-start = (f32[256,2048]{1,0:T(8,128)S(1)}, f32[256,2048]{1,0:T(8,128)}, u32[]{:S(2)}) copy-start(f32[256,2048]{1,0:T(8,128)} %get-tuple-element.68) | copy-start | bytes 6291460
  233.1 1.3 copy-start.4
